TPU v7x, 256 devices: a whole 4x4x8 slice. The times are simulated.
256 devices in a mesh: state: 256 (over y, z, x, core).
Axes of the slice: x: 4, y: 4, z: 8, core: 2. Of those that a mesh axis runs over, the one named last changes fastest.
Arguments:
- transitions: float32 [4096, 16, 4096], P('state'), may hold values from 0 to 1, as said below
- costs: float32 [4096, 16, 128], P('state'), may hold values from 0 to 4
- valid_counts: int32 [4096], P('state'), may hold values from 1 to 16
- start_values: float32 [4096, 128], P('state'), may hold values from -12 to 12
- ref_state: int32 [1], replicated, may hold values from 0 to 4095
Outputs:
- relative_values: float32 [4096, 128], P('state')
- lower_bounds: float32 [4, 128], replicated
- upper_bounds: float32 [4, 128], replicated
Inputs may be any that keep to these rules, and one draw needn't show every extreme that they name: Every entry is nonnegative and each row transitions[s, a, :] sums to one up to float32 rounding. Actions 0 to valid_counts[s] - 1 are allowed in state s.
All inputs are finite; a program needn't handle non-finite values.
Results may differ from a plain program's by a relative error of at most 0.00017.
Values sent between devices are 32-bit elements; how exact they have to be, the bound alone decides.
No kernel may reach another device: no remote copies, remote signals or barrier semaphores. Data moves between devices by JAX's collectives and lax.ppermute only.
A program may use at most 64 MiB of HBM per device.

v0:
```python
import jax
import jax.numpy as jnp
from jax import lax
from jax.sharding import Mesh
from jax.sharding import PartitionSpec as P

ITERS = 4
STATE = ("state_0", "state_1", "state_2", "state_3")
big_value = 1e30


def over_axes(x, axes):
    for axis in axes:
        x = lax.pmax(x, axis)
    return x


def local(transitions, costs, valid_counts, start_values, ref_state):
    local_states = transitions.shape[0]
    actions = transitions.shape[1]
    scenarios = start_values.shape[1]
    flat_rows = transitions.reshape(local_states * actions, transitions.shape[2])
    allowed = jnp.arange(actions, dtype=jnp.int32)[None, :] < valid_counts[:, None]
    my_index = lax.axis_index(STATE)
    first_state = my_index * local_states
    owner_index = ref_state[0] // local_states
    offset = jnp.clip(ref_state[0] - first_state, 0, local_states - 1)
    is_owner = owner_index == my_index
    lower_list = []
    upper_list = []
    unshifted = start_values
    for iteration in range(ITERS):
        field_all = lax.all_gather(unshifted, STATE, axis=0, tiled=True)
        bellman_expected = jnp.dot(
            flat_rows,
            field_all,
            precision=lax.Precision.HIGHEST,
            preferred_element_type=jnp.float32,
        )
        q_values = costs + bellman_expected.reshape(local_states, actions, scenarios)
        q_values = jnp.where(allowed[:, :, None], q_values, jnp.float32(big_value))
        best_value = jnp.min(q_values, axis=1)
        increase = best_value - unshifted
        lower_list.append(jnp.min(increase, axis=0))
        upper_list.append(jnp.max(increase, axis=0))
        unshifted = best_value
    local_row = lax.dynamic_slice_in_dim(unshifted, offset, 1, 0)
    masked_row = jnp.where(is_owner, local_row, jnp.float32(-big_value))
    ref_row, upper_all, negated_all = (
        over_axes(masked_row, STATE),
        over_axes(jnp.stack(upper_list), STATE),
        over_axes(-jnp.stack(lower_list), STATE),
    )
    return (unshifted - ref_row, -negated_all, upper_all)


def solution(mesh):
    split = Mesh(mesh.devices.reshape(4, 8, 4, 2), ("state_0", "state_1", "state_2", "state_3"))
    return jax.shard_map(
        local,
        mesh=split,
        in_specs=(P(STATE, None, None), P(STATE, None, None), P(STATE), P(STATE, None), P()),
        out_specs=(P(STATE, None), P(), P()),
        check_vma=False,
    )
```

profile of v0, /device:TPU:1, one launch (start us, length us, event | category | flops | bytes accessed | tf_op | source)
XLA Modules:
  0.0 506.4 jit_solution(16758565774394789343)
XLA Ops:
  7.2 0.0 all-gather.5.cloned.1.call-start
  7.2 0.7 all-gather.5.cloned.1.call-update
  7.9 0.0 all-gather.7.cloned.1.call-start
  7.9 0.7 iota_compare_fusion
  8.7 111.4 %all-gather.5.cloned.1.call-done = f32[4096,128]{1,0:T(8,128)} async-done(((f32[16,128]{1,0:T(8,128)}), f32[4096,128]{1,0:T(8,128)}) %all-gather.5.cloned.1.call-update) | async-done | bytes 2097168 | tf_op jit(solution)/shard_map/all_gather | solution.py:33
  120.0 6.9 %fusion.8 = f32[16,128]{1,0:T(8,128)} fusion(f32[16,16,128]{2,1,0:T(8,128)} %param.6, f32[16,16,4096]{2,1,0:T(8,128)} %param.5, f32[4096,128]{1,0:T(8,128)} %all-gather.5.cloned.1.call-done, pred[16,16]{1,0:T(8,128)(4,1)S(1)} %iota_compare_fusion), kind=kOutput, calls=%fused_computation.7 | convolution fusion | flops 1610708992 | bytes 6430976 | tf_op jit(solution)/shard_map/dot_general | solution.py:34
  127.0 0.0 all-gather.7.cloned.1.call-update
  127.0 0.0 all-gather.9.cloned.1.call-start
  127.1 103.3 %all-gather.7.cloned.1.call-done = f32[4096,128]{1,0:T(8,128)} async-done(((f32[16,128]{1,0:T(8,128)}), f32[4096,128]{1,0:T(8,128)}) %all-gather.7.cloned.1.call-update) | async-done | bytes 2097168 | tf_op jit(solution)/shard_map/all_gather | solution.py:33
  230.3 6.3 %convolution_bitcast_fusion.2 = f32[256,128]{0,1:T(8,128)S(1)} fusion(f32[4096,128]{1,0:T(8,128)} %all-gather.7.cloned.1.call-done, f32[256,4096]{1,0:T(8,128)} %bitcast.44), kind=kOutput, calls=%fused_computation.6 | convolution fusion | flops 1610612736 | bytes 6422528 | tf_op jit(solution)/shard_map/dot_general | solution.py:34
  236.6 0.1 copy.8
  236.7 0.0 copy-done
  236.8 0.7 select_reduce_fusion.2
  237.5 0.0 all-gather.9.cloned.1.call-update
  237.5 0.2 all-gather.11.cloned.1.call-start
  237.7 103.1 %all-gather.9.cloned.1.call-done = f32[4096,128]{1,0:T(8,128)} async-done(((f32[16,128]{1,0:T(8,128)}), f32[4096,128]{1,0:T(8,128)}) %all-gather.9.cloned.1.call-update) | async-done | bytes 2097168 | tf_op jit(solution)/shard_map/all_gather | solution.py:33
  340.8 6.3 %convolution_bitcast_fusion.1 = f32[256,128]{0,1:T(8,128)S(1)} fusion(f32[4096,128]{1,0:T(8,128)} %all-gather.9.cloned.1.call-done, f32[256,4096]{1,0:T(8,128)} %bitcast.45), kind=kOutput, calls=%fused_computation.5 | convolution fusion | flops 1610612736 | bytes 6422528 | tf_op jit(solution)/shard_map/dot_general | solution.py:34
  347.1 0.1 copy.9
  347.2 0.7 select_reduce_fusion.1
  347.9 0.0 all-gather.11.cloned.1.call-update
  348.6 0.0 copy-start.1
  348.6 0.0 copy-start.4
  348.6 102.6 %all-gather.11.cloned.1.call-done = f32[4096,128]{1,0:T(8,128)} async-done(((f32[16,128]{1,0:T(8,128)}), f32[4096,128]{1,0:T(8,128)}) %all-gather.11.cloned.1.call-update) | async-done | bytes 2097168 | tf_op jit(solution)/shard_map/all_gather | solution.py:33
  451.2 6.3 %convolution_bitcast_fusion = f32[256,128]{0,1:T(8,128)S(1)} fusion(f32[4096,128]{1,0:T(8,128)} %all-gather.11.cloned.1.call-done, f32[256,4096]{1,0:T(8,128)} %bitcast.46), kind=kOutput, calls=%fused_computation.4 | convolution fusion | flops 1610612736 | bytes 6422528 | tf_op jit(solution)/shard_map/dot_general | solution.py:34
  457.5 0.1 copy.10
  457.6 0.1 select_reduce_fusion
  457.8 8.5 %all-reduce.2 = (f32[1,128]{1,0:T(1,128)S(1)}, f32[4,128]{1,0:T(4,128)S(1)}, f32[4,128]{1,0:T(4,128)S(1)}) all-reduce(f32[1,128]{1,0:T(1,128)S(1)} %broadcast_select_fusion, f32[4,128]{1,0:T(4,128)S(1)} %get-tuple-element.29, ...), channel_id=1, replica_groups=mesh['state_0'=4,'state_1'=8,'state_2'=4,'state_3'=2] {'state_0'}, use_global_device_ids=true, to_apply=%region_4.5 | all-reduce | flops 1152 | bytes 9216 | tf_op jit(solution)/shard_map/pmax | solution.py:14
  466.4 13.0 %all-reduce = (f32[1,128]{1,0:T(1,128)S(1)}, f32[4,128]{1,0:T(4,128)S(1)}, f32[4,128]{1,0:T(4,128)S(1)}) all-reduce(f32[1,128]{1,0:T(1,128)S(1)} %get-tuple-element.23, f32[4,128]{1,0:T(4,128)S(1)} %get-tuple-element.24, f32[4,128]{1,0:T(4,128)S(1)} %get-tuple-element.25), channel_id=1, replica_groups=mesh['state_0'=4,'state_1'=8,'state_2'=4,'state_3'=2] {'state_1'}, use_global_device_ids=true, to_apply=%region_5.6 | all-reduce | flops 1152 | bytes 9216 | tf_op jit(solution)/shard_map/pmax | solution.py:14
  479.4 8.5 %all-reduce.1 = (f32[1,128]{1,0:T(1,128)S(1)}, f32[4,128]{1,0:T(4,128)S(1)}, f32[4,128]{1,0:T(4,128)S(1)}) all-reduce(f32[1,128]{1,0:T(1,128)S(1)} %get-tuple-element.17, f32[4,128]{1,0:T(4,128)S(1)} %get-tuple-element.18, f32[4,128]{1,0:T(4,128)S(1)} %get-tuple-element.19), channel_id=1, replica_groups=mesh['state_0'=4,'state_1'=8,'state_2'=4,'state_3'=2] {'state_2'}, use_global_device_ids=true, to_apply=%region_6.7 | all-reduce | flops 1152 | bytes 9216 | tf_op jit(solution)/shard_map/pmax | solution.py:14
  487.9 10.8 %all-reduce.3 = (f32[128]{0:T(128)S(1)}, f32[4,128]{1,0:T(4,128)S(1)}, f32[4,128]{1,0:T(4,128)}) all-reduce(f32[128]{0:T(128)S(1)} %bitcast.55, f32[4,128]{1,0:T(4,128)S(1)} %get-tuple-element.21, f32[4,128]{1,0:T(4,128)S(1)} %get-tuple-element.22), channel_id=1, replica_groups=mesh['state_0'=4,'state_1'=8,'state_2'=4,'state_3'=2] {'state_3'}, use_global_device_ids=true, to_apply=%region_7.8 | all-reduce | flops 1152 | bytes 9216 | tf_op jit(solution)/shard_map/pmax | solution.py:14
  498.7 0.6 broadcast_subtract_fusion
  499.3 0.6 neg.7
  (10 shorter events, 0.1 us)
Async XLA Ops:
  7.2 112.9 %all-gather.5.cloned.1.call-start = ((), (), s32[]{:S(2)}) async-start(), calls=%async_computation | async-start | bytes 2105344 | tf_op jit(solution)/shard_map/all_gather | solution.py:33
  7.9 222.4 %all-gather.7.cloned.1.call-start = ((), (), s32[]{:S(2)}) async-start(), calls=%async_computation.1 | async-start | bytes 2105344 | tf_op jit(solution)/shard_map/all_gather | solution.py:33
  127.0 213.8 %all-gather.9.cloned.1.call-start = ((), (), s32[]{:S(2)}) async-start(), calls=%async_computation.2 | async-start | bytes 2105344 | tf_op jit(solution)/shard_map/all_gather | solution.py:33
  230.3 6.4 %copy-start = (f32[16,16,128]{2,1,0:T(8,128)S(1)}, f32[16,16,128]{2,1,0:T(8,128)}, u32[]{:S(2)}) copy-start(f32[16,16,128]{2,1,0:T(8,128)} %param.6) | copy-start | bytes 393220
  237.5 213.7 %all-gather.11.cloned.1.call-start = ((), (), s32[]{:S(2)}) async-start(), calls=%async_computation.3 | async-start | bytes 2105344 | tf_op jit(solution)/shard_map/all_gather | solution.py:33
  348.6 109.1 %copy-start.1 = (f32[16,128]{1,0:T(8,128)S(1)}, f32[16,128]{1,0:T(8,128)}, u32[]{:S(2)}) copy-start(f32[16,128]{1,0:T(8,128)} %fusion.8) | copy-start | bytes 24580
  348.6 109.1 %copy-start.2 = (f32[16,128]{1,0:T(8,128)S(1)}, f32[16,128]{1,0:T(8,128)}, u32[]{:S(2)}) copy-start(f32[16,128]{1,0:T(8,128)} %select_reduce_fusion.2) | copy-start | bytes 24580
  348.6 109.1 %copy-start.3 = (f32[16,128]{1,0:T(8,128)S(1)}, f32[16,128]{1,0:T(8,128)}, u32[]{:S(2)}) copy-start(f32[16,128]{1,0:T(8,128)} %select_reduce_fusion.1) | copy-start | bytes 24580
  348.6 109.1 %copy-start.4 = (f32[16,128]{1,0:T(8,128)S(1)}, f32[16,128]{1,0:T(8,128)}, u32[]{:S(2)}) copy-start(f32[16,128]{1,0:T(8,128)} %param.8) | copy-start | bytes 24580
Sparse Core Ops, SparseCore 0:
  11.7 108.2 all-gather.4
  127.1 103.1 all-gather.6
  237.6 103.1 all-gather.8
  348.0 103.1 all-gather.10
where the time goes:
time: 507 us; the launch traced here: 506 us
  waiting for transfers between devices  421 us (83%)
  blocking collectives  40.9 us (8%)
  matrix products  25.8 us (5%)
  between operations  14.6 us (3%)
    all_gather x4, waiting for transfers between devices, local(): field_all = lax.all_gather(unshifted, STATE, axis=0, tiled=True)  420 us
    pmax x4, blocking collectives, over_axes(): x = lax.pmax(x, axis)  40.9 us
    dot_general x4, matrix products, local(): jnp.dot(flat_rows, field_all, precision=lax.Precision.HIGHEST, preferred_...  25.8 us
  transfers between devices with their start and end apart: 4, of which 4 were waited for; matrix products, arithmetic and copies ran while one was open for 0% of the time, Pallas kernels for 0%

commit v1 on v0

--- a/solution.py
+++ b/solution.py
@@ -30,7 +30,9 @@
     upper_list = []
     unshifted = start_values
     for iteration in range(ITERS):
-        field_all = lax.all_gather(unshifted, STATE, axis=0, tiled=True)
+        field_all = jnp.concatenate(
+            lax.all_to_all(jnp.stack([unshifted] * lax.axis_size(STATE)), STATE, 0, 0), axis=0
+        )
         bellman_expected = jnp.dot(
             flat_rows,
             field_all,

time: 507 us -> 310 us (0.61)
  waiting for transfers between devices: 421 us -> 106 us
  blocking collectives: 40.9 us -> 156 us
  starting transfers between devices: 0.34 us -> 22.1 us
  between operations: 14.6 us -> 1.5 us
  matrix products: 25.8 us -> 18.5 us
    all_gather x4 -> x0, waiting for transfers between devices: 420 us -> none  [local(): field_all = lax.all_gather(unshifted, STATE, axis=0, tiled=True)]
    all_to_all x0 -> x2, blocking collectives: none -> 119 us  [local(): lax.all_to_all(jnp.stack([unshifted] * lax.axis_size(STATE)), STATE, 0, 0)]
    all_to_all x0 -> x2, waiting for transfers between devices: none -> 106 us  [local(): lax.all_to_all(jnp.stack([unshifted] * lax.axis_size(STATE)), STATE, 0, 0)]
    all_to_all x0 -> x2, starting transfers between devices: none -> 22.1 us  [local(): lax.all_to_all(jnp.stack([unshifted] * lax.axis_size(STATE)), STATE, 0, 0)]
    dot_general x4, matrix products: 25.8 us -> 18.5 us  [local(): jnp.dot(flat_rows, field_all, precision=lax.Precision.HIGHEST, preferred_...]
  transfers between devices with their start and end apart: 4 -> 2, of which waited for: 4 -> 2; matrix products, arithmetic and copies ran while one was open for 0% -> 0% of each run, Pallas kernels for 0% -> 0%
where the time goes in v1:
time: 310 us
  blocking collectives  156 us (50%)
  waiting for transfers between devices  106 us (34%)
  starting transfers between devices  22.1 us (7%)
  matrix products  18.5 us (6%)
  local copies, waits for them, and re-layouts  4.23 us (1%)
    all_to_all x2, blocking collectives, local(): lax.all_to_all(jnp.stack([unshifted] * lax.axis_size(STATE)), STATE, 0, 0)  119 us
    all_to_all x2, waiting for transfers between devices, local(): lax.all_to_all(jnp.stack([unshifted] * lax.axis_size(STATE)), STATE, 0, 0)  106 us
    pmax x4, blocking collectives, over_axes(): x = lax.pmax(x, axis)  36.8 us
    all_to_all x2, starting transfers between devices, local(): lax.all_to_all(jnp.stack([unshifted] * lax.axis_size(STATE)), STATE, 0, 0)  22.1 us
    dot_general x4, matrix products, local(): jnp.dot(flat_rows, field_all, precision=lax.Precision.HIGHEST, preferred_...  18.5 us
  transfers between devices with their start and end apart: 2, of which 2 were waited for; matrix products, arithmetic and copies ran while one was open for 0% of the time, Pallas kernels for 0%

profile of v1, /device:TPU:1, one launch (start us, length us, event | category | flops | bytes accessed | tf_op | source)
XLA Modules:
  0.0 309.7 jit_solution(7165057655994753762)
XLA Ops:
  0.6 2.2 stack.28
  2.8 15.6 %all-to-all-start = ((f32[256,16,128]{2,1,0:T(8,128)}), f32[256,16,128]{2,1,0:T(8,128)S(1)}, u32[]{:S(2)}, u32[]{:S(2)}) async-start(f32[256,16,128]{2,1,0:T(8,128)} %stack.28), calls=%async_computation | async-start | bytes 4194304 | tf_op jit(solution)/shard_map/all_to_all | solution.py:34
  18.5 0.0 copy-done.4
  18.5 0.1 iota_compare_fusion
  18.6 53.2 %all-to-all-done = f32[256,16,128]{2,1,0:T(8,128)S(1)} async-done(((f32[256,16,128]{2,1,0:T(8,128)}), f32[256,16,128]{2,1,0:T(8,128)S(1)}, u32[]{:S(2)}, u32[]{:S(2)}) %all-to-all-start) | async-done | bytes 2097184 | tf_op jit(solution)/shard_map/all_to_all | solution.py:34
  71.8 0.0 copy-done.2
  71.8 5.7 %fusion.1 = f32[16,128]{1,0:T(8,128)S(1)} fusion(f32[16,16,128]{2,1,0:T(8,128)S(1)} %copy-done.2, f32[16,16,4096]{2,1,0:T(8,128)} %param.5, f32[4096,128,1]{1,0,2:T(8,128)S(1)} %bitcast.46, pred[16,16]{1,0:T(8,128)(4,1)S(1)} %iota_compare_fusion), kind=kOutput, calls=%fused_computation.5 | convolution fusion | flops 1610708992 | bytes 6430976 | tf_op jit(solution)/shard_map/dot_general | solution.py:36
  77.5 0.1 stack.29
  77.7 0.0 copy-start
  77.7 59.5 %all_to_all.20 = f32[256,16,128]{2,1,0:T(8,128)S(1)} all-to-all(f32[256,16,128]{2,1,0:T(8,128)S(1)} %stack.29), channel_id=1, replica_groups=mesh['state_0'=4,'state_1'=8,'state_2'=4,'state_3'=2] {'state_0','state_..., dimensions={0} | all-to-all | bytes 4194304 | tf_op jit(solution)/shard_map/all_to_all | solution.py:34
  137.2 0.0 copy-done
  137.2 3.6 %convolution_bitcast_fusion.2 = f32[256,128]{0,1:T(8,128)S(1)} fusion(f32[4096,128]{1,0:T(8,128)S(1)} %bitcast.47, f32[256,4096]{1,0:T(8,128)S(1)} %bitcast.43), kind=kOutput, calls=%fused_computation.2 | convolution fusion | flops 1610612736 | bytes 6422528 | tf_op jit(solution)/shard_map/dot_general | solution.py:36
  140.8 0.1 copy.8
  140.9 0.1 select_reduce_fusion.2
  141.0 0.1 stack.30
  141.2 0.0 copy-start.1
  141.2 59.5 %all_to_all.21 = f32[256,16,128]{2,1,0:T(8,128)S(1)} all-to-all(f32[256,16,128]{2,1,0:T(8,128)S(1)} %stack.30), channel_id=1, replica_groups=mesh['state_0'=4,'state_1'=8,'state_2'=4,'state_3'=2] {'state_0','state_..., dimensions={0} | all-to-all | bytes 4194304 | tf_op jit(solution)/shard_map/all_to_all | solution.py:34
  200.7 3.6 %convolution_bitcast_fusion.1 = f32[256,128]{0,1:T(8,128)S(1)} fusion(f32[4096,128]{1,0:T(8,128)S(1)} %bitcast.48, f32[256,4096]{1,0:T(8,128)S(1)} %bitcast.44), kind=kOutput, calls=%fused_computation.1 | convolution fusion | flops 1610612736 | bytes 6422528 | tf_op jit(solution)/shard_map/dot_general | solution.py:36
  204.3 0.1 copy.9
  204.4 0.1 select_reduce_fusion.1
  204.5 1.5 stack.31
  206.0 6.4 %all-to-all-start.3 = ((f32[256,16,128]{2,1,0:T(8,128)}), f32[256,16,128]{2,1,0:T(8,128)S(1)}, u32[]{:S(2)}, u32[]{:S(2)}) async-start(f32[256,16,128]{2,1,0:T(8,128)} %stack.31), calls=%async_computation.3 | async-start | bytes 4194304 | tf_op jit(solution)/shard_map/all_to_all | solution.py:34
  213.1 52.6 %all-to-all-done.3 = f32[256,16,128]{2,1,0:T(8,128)S(1)} async-done(((f32[256,16,128]{2,1,0:T(8,128)}), f32[256,16,128]{2,1,0:T(8,128)S(1)}, u32[]{:S(2)}, u32[]{:S(2)}) %all-to-all-start.3) | async-done | bytes 2097184 | tf_op jit(solution)/shard_map/all_to_all | solution.py:34
  265.8 5.7 %convolution_bitcast_fusion = f32[256,128]{0,1:T(8,128)S(1)} fusion(f32[4096,128]{1,0:T(8,128)S(1)} %bitcast.45, f32[256,4096]{1,0:T(8,128)} %bitcast.42), kind=kOutput, calls=%fused_computation | convolution fusion | flops 1610612736 | bytes 6422528 | tf_op jit(solution)/shard_map/dot_general | solution.py:36
  271.4 0.1 copy.10
  271.5 0.1 select_reduce_fusion
  271.7 6.8 %all-reduce.2 = (f32[1,128]{1,0:T(1,128)S(1)}, f32[4,128]{1,0:T(4,128)S(1)}, f32[4,128]{1,0:T(4,128)S(1)}) all-reduce(f32[1,128]{1,0:T(1,128)S(1)} %broadcast_select_fusion, f32[4,128]{1,0:T(4,128)S(1)} %get-tuple-element.29, ...), channel_id=1, replica_groups=mesh['state_0'=4,'state_1'=8,'state_2'=4,'state_3'=2] {'state_0'}, use_global_device_ids=true, to_apply=%region_4.5 | all-reduce | flops 1152 | bytes 9216 | tf_op jit(solution)/shard_map/pmax | solution.py:14
  278.6 11.4 %all-reduce = (f32[1,128]{1,0:T(1,128)S(1)}, f32[4,128]{1,0:T(4,128)S(1)}, f32[4,128]{1,0:T(4,128)S(1)}) all-reduce(f32[1,128]{1,0:T(1,128)S(1)} %get-tuple-element.23, f32[4,128]{1,0:T(4,128)S(1)} %get-tuple-element.24, f32[4,128]{1,0:T(4,128)S(1)} %get-tuple-element.25), channel_id=1, replica_groups=mesh['state_0'=4,'state_1'=8,'state_2'=4,'state_3'=2] {'state_1'}, use_global_device_ids=true, to_apply=%region_5.6 | all-reduce | flops 1152 | bytes 9216 | tf_op jit(solution)/shard_map/pmax | solution.py:14
  289.9 7.4 %all-reduce.1 = (f32[1,128]{1,0:T(1,128)S(1)}, f32[4,128]{1,0:T(4,128)S(1)}, f32[4,128]{1,0:T(4,128)S(1)}) all-reduce(f32[1,128]{1,0:T(1,128)S(1)} %get-tuple-element.17, f32[4,128]{1,0:T(4,128)S(1)} %get-tuple-element.18, f32[4,128]{1,0:T(4,128)S(1)} %get-tuple-element.19), channel_id=1, replica_groups=mesh['state_0'=4,'state_1'=8,'state_2'=4,'state_3'=2] {'state_2'}, use_global_device_ids=true, to_apply=%region_6.7 | all-reduce | flops 1152 | bytes 9216 | tf_op jit(solution)/shard_map/pmax | solution.py:14
  297.4 11.1 %all-reduce.3 = (f32[128]{0:T(128)S(1)}, f32[4,128]{1,0:T(4,128)S(1)}, f32[4,128]{1,0:T(4,128)}) all-reduce(f32[128]{0:T(128)S(1)} %bitcast.57, f32[4,128]{1,0:T(4,128)S(1)} %get-tuple-element.21, f32[4,128]{1,0:T(4,128)S(1)} %get-tuple-element.22), channel_id=1, replica_groups=mesh['state_0'=4,'state_1'=8,'state_2'=4,'state_3'=2] {'state_3'}, use_global_device_ids=true, to_apply=%region_7.8 | all-reduce | flops 1152 | bytes 9216 | tf_op jit(solution)/shard_map/pmax | solution.py:14
  308.5 0.6 broadcast_subtract_fusion
  309.1 0.6 neg.7
  (8 shorter events, 0.1 us)
Async XLA Ops:
  2.8 15.7 %copy-start.4 = (s32[16]{0:T(128)S(1)}, s32[16]{0:T(128)}, u32[]{:S(2)}) copy-start(s32[16]{0:T(128)} %param.7) | copy-start | bytes 196
  2.8 69.0 %copy-start.2 = (f32[16,16,128]{2,1,0:T(8,128)S(1)}, f32[16,16,128]{2,1,0:T(8,128)}, u32[]{:S(2)}) copy-start(f32[16,16,128]{2,1,0:T(8,128)} %param.6) | copy-start | bytes 393220
  2.8 69.0 %all-to-all-start = ((f32[256,16,128]{2,1,0:T(8,128)}), f32[256,16,128]{2,1,0:T(8,128)S(1)}, u32[]{:S(2)}, u32[]{:S(2)}) async-start(f32[256,16,128]{2,1,0:T(8,128)} %stack.28), calls=%async_computation | async-start | bytes 4194304 | tf_op jit(solution)/shard_map/all_to_all | solution.py:34
  77.7 59.6 %copy-start = (f32[16,16,4096]{2,1,0:T(8,128)S(1)}, f32[16,16,4096]{2,1,0:T(8,128)}, u32[]{:S(2)}) copy-start(f32[16,16,4096]{2,1,0:T(8,128)} %param.5) | copy-start | bytes 12582916
  141.2 59.6 %copy-start.1 = (f32[16,16,4096]{2,1,0:T(8,128)S(1)}, f32[16,16,4096]{2,1,0:T(8,128)}, u32[]{:S(2)}) copy-start(f32[16,16,4096]{2,1,0:T(8,128)} %param.5) | copy-start | bytes 12582916
  206.0 59.7 %all-to-all-start.3 = ((f32[256,16,128]{2,1,0:T(8,128)}), f32[256,16,128]{2,1,0:T(8,128)S(1)}, u32[]{:S(2)}, u32[]{:S(2)}) async-start(f32[256,16,128]{2,1,0:T(8,128)} %stack.31), calls=%async_computation.3 | async-start | bytes 4194304 | tf_op jit(solution)/shard_map/all_to_all | solution.py:34
  265.8 5.9 %copy-start.3 = (f32[16,128]{1,0:T(8,128)S(1)}, f32[16,128]{1,0:T(8,128)}, u32[]{:S(2)}) copy-start(f32[16,128]{1,0:T(8,128)} %param.8) | copy-start | bytes 24580
